TPU v7x, 32 devices: a whole 2x2x4 slice. The times are simulated.
32 devices in a mesh: dp: 8 (over z, y), tensor: 4 (over x, core).
Axes of the slice: x: 2, y: 2, z: 4, core: 2. Of those that a mesh axis runs over, the one named last changes fastest.
Arguments:
- patches: bfloat16 [8192, 1280], P('dp'), may hold values from -27 to 27
- norm_gain: float32 [1280], replicated, may hold values from 0.1 to 1.9
- norm_bias: float32 [1280], replicated, may hold values from -3 to 3
- first_weight: bfloat16 [5120, 5120], P(None, 'tensor'), may hold values from -0.078125 to 0.078125
- first_bias: float32 [5120], P('tensor'), may hold values from -3 to 3
- second_weight: bfloat16 [5120, 8192], P('tensor', 'dp'), may hold values from -0.078125 to 0.078125
- second_bias: float32 [8192], P('tensor'), may hold values from -2 to 2
- text_embeds: bfloat16 [4096, 8192], P('dp', 'tensor'), may hold values from -36 to 36
- final_gain: float32 [8192], P('tensor'), may hold values from 0.1 to 1.9
- image_grids: int32 [8, 4, 2], replicated, may hold values from 2 to 8, as said below
- routing: int32 [8, 4], replicated, may hold values from 0 to 3, each once within a row
Outputs:
- embeddings: bfloat16 [4096, 8192], P('dp', 'tensor')
- normed: bfloat16 [4096, 8192], P('dp', 'tensor')
Inputs may be any that keep to these rules, and one draw needn't show every extreme that they name: `image_grids`: each image is a grid of 3 to 8 rows by 2 to 8 columns of merged tokens; in every draw some image is 8 by 8. `routing`: each row names every offset 0 to 3 once.
All inputs are finite; a program needn't handle non-finite values.
Results may differ from a plain program's by a relative error of at most 0.006.
Values may be sent and summed in bfloat16 or wider, within the bound.
A program may use at most 128 MiB of HBM per device.

v0:
```python
import functools

import jax
import jax.numpy as jnp
from jax import lax
from jax.experimental import pallas as pl
from jax.experimental.pallas import tpu as pltpu
from jax.sharding import PartitionSpec as P

VMEM_LIMIT = 56 * 1024 * 1024


def hidden_kernel(per_token, patches_ref, gain_ref, bias_ref, weight_ref, first_bias_ref, index_ref, out_ref, rows_ref, total_ref):
    step = pl.program_id(0)
    tokens = out_ref.shape[0]

    @pl.when(step == 0)
    def _():
        gain = gain_ref[...][None, :]
        bias = bias_ref[...][None, :]

        def chunk(i, carry):
            span = pl.ds(pl.multiple_of(i * 128, 128), 128)
            values = patches_ref[span, :].astype(jnp.float32)
            centered = values - jnp.mean(values, axis=-1, keepdims=True)
            variance = jnp.mean(centered * centered, axis=-1, keepdims=True)
            normed = centered * lax.rsqrt(variance + 1e-06) * gain + bias
            for c in range(normed.shape[1] // 128):
                rows_ref[c, span, :] = normed[:, c * 128:(c + 1) * 128]
            return carry

        lax.fori_loop(0, patches_ref.shape[0] // 128, chunk, 0)
        total_ref[...] = jnp.zeros_like(total_ref)

    strips = [rows_ref[c, pl.ds(step, tokens, stride=per_token), :] for c in range(rows_ref.shape[0])]
    merged = jnp.concatenate(strips, axis=1).astype(jnp.bfloat16)
    total_ref[...] += jnp.dot(merged, weight_ref[...], preferred_element_type=jnp.float32)

    @pl.when(step == per_token - 1)
    def _():
        x = total_ref[...] + first_bias_ref[...][None, :]
        hidden = (0.5 * x * (1.0 + lax.erf(x * (0.5 ** 0.5)))).astype(jnp.bfloat16)
        columns = lax.broadcasted_iota(jnp.int32, (tokens, tokens), 1)
        pick = (columns == index_ref[...]).astype(jnp.bfloat16)
        out_ref[...] = jnp.dot(pick, hidden, preferred_element_type=jnp.float32).astype(jnp.bfloat16)


def compact_hidden(patches, norm_gain, norm_bias, first_weight, first_bias, index):
    width = patches.shape[1]
    per_token = first_weight.shape[0] // width
    tokens = patches.shape[0] // per_token
    out_width = first_weight.shape[1]
    whole = lambda shape: pl.BlockSpec(shape, lambda j: (0,) * len(shape))
    return pl.pallas_call(
        functools.partial(hidden_kernel, per_token),
        grid=(per_token,),
        in_specs=[
            whole(patches.shape),
            whole((width,)),
            whole((width,)),
            pl.BlockSpec((width, out_width), lambda j: (j, 0)),
            whole((out_width,)),
            whole((tokens, 1)),
        ],
        out_specs=whole((tokens, out_width)),
        out_shape=jax.ShapeDtypeStruct((tokens, out_width), jnp.bfloat16),
        scratch_shapes=[
            pltpu.VMEM((width // 128, patches.shape[0], 128), jnp.float32),
            pltpu.VMEM((tokens, out_width), jnp.float32),
        ],
        compiler_params=pltpu.CompilerParams(vmem_limit_bytes=VMEM_LIMIT),
        cost_estimate=pl.CostEstimate(
            flops=2 * tokens * first_weight.size, bytes_accessed=2 * first_weight.size, transcendentals=0
        ),
        name="compact_hidden",
    )(patches, norm_gain, norm_bias, first_weight, first_bias, index[:, None])


def project_kernel(strides, *refs):
    index_ref, weight_ref, out_ref = refs[strides], refs[strides + 1], refs[strides + 2]
    rows = out_ref.shape[1]
    index = index_ref[0]
    columns = lax.broadcasted_iota(jnp.int32, (rows, rows), 1)
    total = None
    for k in range(strides):
        pick = (columns + k * rows == index).astype(jnp.bfloat16)
        term = jnp.dot(pick, refs[k][0], preferred_element_type=jnp.float32)
        total = term if total is None else total + term
    out_ref[0] = jnp.dot(total.astype(jnp.bfloat16), weight_ref[...], preferred_element_type=jnp.float32).astype(jnp.bfloat16)


def project(gathered, second_weight, index, strides):
    shards, rows, depth = gathered.shape
    width = second_weight.shape[1]
    source = lambda k: pl.BlockSpec((1, rows, depth), lambda e: ((e + shards - k) % shards, 0, 0))
    return pl.pallas_call(
        functools.partial(project_kernel, strides),
        grid=(shards,),
        in_specs=[source(k) for k in range(strides)]
        + [pl.BlockSpec((1, rows, 1), lambda e: (e, 0, 0)), pl.BlockSpec((depth, width), lambda e: (0, 0))],
        out_specs=pl.BlockSpec((1, rows, width), lambda e: (e, 0, 0)),
        out_shape=jax.ShapeDtypeStruct((shards, rows, width), jnp.bfloat16),
        compiler_params=pltpu.CompilerParams(vmem_limit_bytes=VMEM_LIMIT),
        cost_estimate=pl.CostEstimate(
            flops=2 * shards * rows * depth * width, bytes_accessed=4 * gathered.size, transcendentals=0
        ),
        name="project",
    )(*([gathered] * strides), index[:, :, None], second_weight)


def gather_kernel(own_ref, out_ref, line_send, line_recv, pair_send, pair_recv):
    shards = out_ref.shape[0]
    length = shards // 2
    me = lax.axis_index("dp")
    place, row = me // 2, me % 2
    other = me + 1 - 2 * row
    barrier = pltpu.get_barrier_semaphore()
    pl.semaphore_signal(barrier, inc=1, device_id={"dp": other})

    @pl.when(place > 0)
    def _():
        pl.semaphore_signal(barrier, inc=1, device_id={"dp": me - 2})

    @pl.when(place < length - 1)
    def _():
        pl.semaphore_signal(barrier, inc=1, device_id={"dp": me + 2})

    peers = 1 + (place > 0).astype(jnp.int32) + (place < length - 1).astype(jnp.int32)
    pl.semaphore_wait(barrier, peers)

    def line_copy(block, way, src):
        return pltpu.make_async_remote_copy(
            src_ref=src,
            dst_ref=out_ref.at[2 * block + row],
            send_sem=line_send.at[(way + 1) // 2, block],
            recv_sem=line_recv.at[block],
            device_id={"dp": me + 2 * way},
        )

    def pair_copy(block, src, side):
        return pltpu.make_async_remote_copy(
            src_ref=src,
            dst_ref=out_ref.at[2 * block + side],
            send_sem=pair_send.at[block],
            recv_sem=pair_recv.at[block],
            device_id={"dp": other},
        )

    for step in range(length):
        for way in (1, -1):
            block = place - way * step
            src = own_ref if step == 0 else out_ref.at[2 * block + row]

            @pl.when((block >= 0) & (block < length))
            def _(way=way, block=block, src=src, step=step):
                if step > 0:
                    line_copy(block, way, src).wait_recv()

                @pl.when((place + way >= 0) & (place + way < length))
                def _():
                    line_copy(block, way, src).start()

                if step > 0 or way == 1:
                    pair_copy(block, src, row).start()

    out_ref[me] = own_ref[...]

    def drain(block, carry):
        here = out_ref.at[2 * block + row]
        pair_copy(block, here, 1 - row).wait_recv()
        pair_copy(block, here, row).wait_send()

        @pl.when((block <= place) & (place < length - 1))
        def _():
            line_copy(block, 1, here).wait_send()

        @pl.when((block >= place) & (place > 0))
        def _():
            line_copy(block, -1, here).wait_send()

        return carry

    lax.fori_loop(0, length, drain, 0)


def gathered_rows(own, call_id):
    shards = lax.axis_size("dp")
    dma = pltpu.SemaphoreType.DMA
    return pl.pallas_call(
        gather_kernel,
        in_specs=[pl.BlockSpec(memory_space=pltpu.VMEM)],
        out_specs=pl.BlockSpec(memory_space=pltpu.VMEM),
        out_shape=jax.ShapeDtypeStruct((shards,) + own.shape, own.dtype),
        scratch_shapes=[dma((2, shards // 2)), dma((shards // 2,)), dma((shards // 2,)), dma((shards // 2,))],
        compiler_params=pltpu.CompilerParams(
            collective_id=call_id, has_side_effects=True, vmem_limit_bytes=VMEM_LIMIT
        ),
        name="gather_rows",
    )(own)


def scatter_kernel(
    part_ref, out_ref, pair_in, cross_out, cross_in, ready, wide,
    pair_send, pair_recv, cross_send, cross_recv, wide_send, wide_recv, out_send, out_recv,
):
    shards, groups = part_ref.shape[0], part_ref.shape[1]
    per_group = shards // groups
    me = lax.axis_index("dp")
    group = lax.axis_index("tensor")
    core, side = group % 2, group // 2
    mate = 2 * side + 1 - core
    across = group + 2 - 4 * side
    across_mate = mate + 2 - 4 * side
    f32 = jnp.float32

    barrier = pltpu.get_barrier_semaphore()
    for peer in (mate, across, across_mate):
        pl.semaphore_signal(barrier, inc=1, device_id={"tensor": peer})

    def greet(i, carry):
        pl.semaphore_signal(barrier, inc=1, device_id={"dp": (me + 1 + i) % shards})
        return carry

    lax.fori_loop(0, shards - 1, greet, 0)
    pl.semaphore_wait(barrier, shards + 2)

    def pair_copy(e, slot):
        return pltpu.make_async_remote_copy(
            src_ref=part_ref.at[e, mate if slot == 0 else across_mate],
            dst_ref=pair_in.at[e, slot],
            send_sem=pair_send.at[slot, e],
            recv_sem=pair_recv.at[slot, e],
            device_id={"tensor": mate},
        )

    def cross_copy(e):
        return pltpu.make_async_remote_copy(
            src_ref=cross_out.at[e],
            dst_ref=cross_in.at[e],
            send_sem=cross_send.at[e],
            recv_sem=cross_recv.at[e],
            device_id={"tensor": across},
        )

    def wide_copy(e, source):
        return pltpu.make_async_remote_copy(
            src_ref=ready.at[e],
            dst_ref=wide.at[source],
            send_sem=wide_send.at[e],
            recv_sem=wide_recv.at[source],
            device_id={"dp": e},
        )

    def out_copy(source, target, sender):
        return pltpu.make_async_remote_copy(
            src_ref=wide.at[source],
            dst_ref=out_ref.at[sender, source % per_group],
            send_sem=out_send.at[source],
            recv_sem=out_recv.at[sender, source % per_group],
            device_id={"tensor": target},
        )

    def start_pair(i, carry):
        e = (me + 1 + i) % shards
        for slot in (1, 0):
            pair_copy(e, slot).start()
        return carry

    lax.fori_loop(0, shards, start_pair, 0)

    def start_cross(i, carry):
        e = (me + 1 + i) % shards
        pair_copy(e, 1).wait_recv()
        cross_out[e] = (part_ref[e, across].astype(f32) + pair_in[e, 1].astype(f32)).astype(jnp.bfloat16)
        cross_copy(e).start()
        return carry

    lax.fori_loop(0, shards, start_cross, 0)

    def forward(source):
        target = source // per_group

        @pl.when(target == group)
        def _():
            out_ref[group, source % per_group] = wide[source]

        @pl.when(target != group)
        def _():
            out_copy(source, target, group).start()

    lag = 2

    def start_wide(i, carry):
        @pl.when(i < shards)
        def _():
            e = (me + 1 + i) % shards
            pair_copy(e, 0).wait_recv()
            cross_copy(e).wait_recv()
            total = part_ref[e, group].astype(f32) + pair_in[e, 0].astype(f32) + cross_in[e].astype(f32)

            @pl.when(i < shards - 1)
            def _():
                ready[e] = total.astype(jnp.bfloat16)
                wide_copy(e, me).start()

            @pl.when(i == shards - 1)
            def _():
                wide[me] = total.astype(jnp.bfloat16)
                forward(me)

        @pl.when((i >= lag) & (i < shards - 1 + lag))
        def _():
            source = (me + 2 * shards - 1 - (i - lag)) % shards
            wide_copy(source, source).wait_recv()
            forward(source)

        return carry

    lax.fori_loop(0, shards + lag - 1, start_wide, 0)

    def drain(i, carry):
        e = (me + 1 + i) % shards
        for slot in (1, 0):
            pair_copy(e, slot).wait_send()
        cross_copy(e).wait_send()

        @pl.when(i < shards - 1)
        def _():
            wide_copy(e, me).wait_send()

        @pl.when(e // per_group != group)
        def _():
            out_copy(e, e // per_group, group).wait_send()

        return carry

    lax.fori_loop(0, shards, drain, 0)
    for peer in (mate, across, across_mate):

        def receive(c, carry, peer=peer):
            out_copy(group * per_group + c, peer, peer).wait_recv()
            return carry

        lax.fori_loop(0, per_group, receive, 0)


def scattered_rows(pieces, call_id):
    shards, groups, rows, width = pieces.shape
    dma = pltpu.SemaphoreType.DMA
    block = pltpu.VMEM((shards, rows, width), jnp.bfloat16)
    out = pl.pallas_call(
        scatter_kernel,
        in_specs=[pl.BlockSpec(memory_space=pltpu.VMEM)],
        out_specs=pl.BlockSpec(memory_space=pltpu.VMEM),
        out_shape=jax.ShapeDtypeStruct((groups, shards // groups, rows, width), jnp.bfloat16),
        scratch_shapes=[
            pltpu.VMEM((shards, 2, rows, width), jnp.bfloat16), block, block, block, block,
            dma((2, shards)), dma((2, shards)), dma((shards,)), dma((shards,)),
            dma((shards,)), dma((shards,)), dma((shards,)), dma((groups, shards // groups)),
        ],
        compiler_params=pltpu.CompilerParams(
            collective_id=call_id, has_side_effects=True, vmem_limit_bytes=VMEM_LIMIT
        ),
        name="scatter_rows",
    )(pieces)
    return out.transpose(0, 2, 1, 3).reshape(groups * rows, -1)


def per_device(
    patches,
    norm_gain,
    norm_bias,
    first_weight,
    first_bias,
    second_weight,
    second_bias,
    text_embeds,
    final_gain,
    image_grids,
    routing,
):
    own_index = lax.axis_index("dp")
    shards = lax.axis_size("dp")
    groups = lax.axis_size("tensor")
    strides = image_grids.shape[1]
    slots = patches.shape[0] * patches.shape[1] // first_weight.shape[0]
    cap = slots // strides
    seq_rows, feature_width = text_embeds.shape
    slot_ids = jnp.arange(strides, dtype=jnp.int32)
    lower = (slot_ids[:, None] < slot_ids[None, :]).astype(jnp.int32)

    is_at = (routing[:, None, :] == slot_ids[None, :, None]).astype(jnp.int32)
    areas = image_grids[:, :, 0] * image_grids[:, :, 1]
    counts = jnp.sum(is_at * areas[:, None, :], axis=-1)
    chosen = jnp.sum(is_at * slot_ids, axis=-1)
    starts = jnp.sum(counts[:, :, None] * lower, axis=1)
    arriving = jnp.stack([jnp.roll(counts[:, k], k) for k in range(strides)], axis=1)
    source_starts = jnp.stack([jnp.roll(starts[:, k], k) for k in range(strides)], axis=1)
    laid_at = jnp.sum(arriving[:, :, None] * lower, axis=1)
    filled = jnp.sum(arriving, axis=1)
    most = jnp.maximum(jnp.max(jnp.sum(counts, axis=1)), jnp.max(filled))

    position = jnp.arange(slots, dtype=jnp.int32)
    own = lambda table: lax.dynamic_index_in_dim(table, own_index, 0, keepdims=False)
    inside = position[:, None] - own(starts)[None, :]
    live = (inside >= 0) & (inside < own(counts)[None, :])
    own_pick = jnp.sum(jnp.where(live, own(chosen)[None, :] * cap + inside + 1, 0), axis=1) - 1
    hidden = compact_hidden(patches, norm_gain, norm_bias, first_weight, first_bias, own_pick)

    def image_part(rows, call_id):
        inside = position[None, :rows, None] - laid_at[:, None, :]
        live = (inside >= 0) & (inside < arriving[:, None, :])
        index = jnp.sum(
            jnp.where(live, slot_ids * rows + source_starts[:, None, :] + inside + 1, 0), axis=2
        ) - 1
        gathered = gathered_rows(hidden[:rows], 2 * call_id)
        partial_value = project(gathered, second_weight, index, strides)
        pieces = partial_value.reshape(shards, groups, rows // groups, -1)
        image_rows = scattered_rows(pieces, 2 * call_id + 1)
        return jnp.pad(image_rows, ((0, slots - rows), (0, 0)))

    buckets = (slots * 3 // 4, slots)
    image_rows = lax.cond(
        most <= buckets[0],
        lambda: image_part(buckets[0], 0),
        lambda: image_part(buckets[1], 1),
    )
    image_rows = (image_rows.astype(jnp.float32) + second_bias).astype(jnp.bfloat16)
    image_rows = jnp.pad(image_rows, ((0, seq_rows - slots), (0, 0)))
    row_ids = jnp.arange(seq_rows, dtype=jnp.int32)[:, None]
    embeddings = jnp.where(row_ids < own(filled), image_rows, text_embeds)
    embed_values = embeddings.astype(jnp.float32)
    square_total = lax.psum(jnp.sum(embed_values * embed_values, axis=-1), "tensor")
    scale_rows = lax.rsqrt(square_total / (feature_width * groups) + 1e-06)
    normed = (embed_values * scale_rows[:, None] * final_gain).astype(jnp.bfloat16)
    return (embeddings, normed)


def solution(mesh):
    placed = (
        P("dp", None),
        P(),
        P(),
        P(None, "tensor"),
        P("tensor"),
        P("tensor", "dp"),
        P("tensor"),
        P("dp", "tensor"),
        P("tensor"),
        P(),
        P(),
    )
    return jax.shard_map(
        per_device,
        mesh=mesh,
        in_specs=placed,
        out_specs=(P("dp", "tensor"), P("dp", "tensor")),
        check_vma=False,
    )
```

profile of v0, /device:TPU:0, one launch (start us, length us, event | category | flops | bytes accessed | tf_op | source)
XLA Modules:
  0.0 140.5 jit_solution(16258685578307755113)
XLA Ops:
  0.7 0.8 slice_multiply_fusion
  1.4 0.7 select_reduce_fusion.1
  2.1 0.6 slice.117
  2.7 0.6 reduce_max.18
  3.4 0.7 fusion.19
  4.2 1.4 %fusion.20 = (s32[]{:T(128)}, s32[8]{0:T(128)S(1)}, s32[8,1]{0,1:T(1,128)S(1)}) fusion(s32[5]{0:T(128)S(1)} %slice_bitcast_fusion.5, s32[3]{0:T(128)S(1)} %slice_bitcast_fusion.6, s32[6]{0:T(128)S(1)} %slice_bitcast_fusion.7, s32[2]{0:T(128)S(1)} %slice_bitcast_fusion.8, s32[7]{0:T(128)S(1)} %slice_bitcast_fusion.9, s32[1]{0:T(128)} %bitcast.8, ...), kind=kLoop, calls=%fused_computation.72 | loop fusion | flops 55 | bytes 196 | tf_op jit(solution)/shard_map/reduce_max | solution.py:401
  7.0 0.2 multiply_reduce_fusion.3
  7.2 0.6 dynamic_slice.14
  7.8 0.6 iota_compare_fusion.2
  8.5 0.1 multiply_reduce_fusion.2
  8.6 0.6 slice.130
  9.2 0.2 dynamic-slice_reduce_fusion.1
  9.3 0.1 select_reduce_fusion.3
  9.5 0.1 add_bitcast_fusion.4
  9.7 0.7 add_bitcast_fusion.2
  10.5 0.8 copy.52.index_ref
  11.3 11.2 %compact_hidden.1 = bf16[256,1280]{1,0:T(8,128)(2,1)S(1)} custom-call(bf16[1024,1280]{1,0:T(8,128)(2,1)} %patches_ref.1, f32[1280]{0:T(1024)} %gain_ref.1, f32[1280]{0:T(1024)} %bias_ref.1, bf16[5120,1280]{1,0:T(8,128)(2,1)} %weight_ref.1, f32[1280]{0:T(1024)} %first_bias_ref.1, s32[256,1]{1,0:T(8,128)} %copy.52.index_ref), custom_call_target="tpu_custom_call" | custom-call | flops 3355443200 | bytes 13107200 | tf_op jit(solution)/shard_map/compact_hidden/pallas_call | solution.py:54
  22.6 107.8 %conditional.6 = (bf16[256,2048]{1,0:T(8,128)(2,1)S(1)}) conditional(s32[]{:T(128)} %convert_element_type.37, (bf16[256,1280]{1,0:T(8,128)(2,1)S(1)}, s32[256]{0:T(256)S(1)}, s32[8,4]{0,1:T(4,128)S(1)}, s32[8,4,4]{0,2,1:T(4,128)S(1)}, s32[4]{0:T(128)S(1)}, /*index=5*/s32[8,4]{0,1:T(4,128)S(1)}, bf16[1280,1024]{1,0:T(8,128)(2,1)S(1)}) %tuple.36, ...), branch_computations={%region_7.10_spmd, %region_10.13_spmd} | conditional | flops 5368775168 | bytes 14723512
  22.6 0.8 slice.84.own_ref
  23.5 0.1 fusion.6
  23.6 1.2 copy.50.refs_4_
  24.8 52.4 %gather_rows.3.refs_0_.refs_1_.refs_2_.refs_3_ = bf16[8,192,1280]{2,1,0:T(8,128)(2,1)} custom-call(bf16[192,1280]{1,0:T(8,128)(2,1)} %slice.84.own_ref), custom_call_target="tpu_custom_call" | custom-call | tf_op jit(solution)/shard_map/cond/branch_1_fun/gather_rows/pallas_call | solution.py:189
  77.2 13.8 %project.3 = bf16[8,192,1024]{2,1,0:T(8,128)(2,1)} custom-call(bf16[8,192,1280]{2,1,0:T(8,128)(2,1)} %gather_rows.3.refs_0_.refs_1_.refs_2_.refs_3_, bf16[8,192,1280]{2,1,0:T(8,128)(2,1)} %gather_rows.3.refs_0_.refs_1_.refs_2_.refs_3_, bf16[8,192,1280]{2,1,0:T(8,128)(2,1)} %gather_rows.3.refs_0_.refs_1_.refs_2_.refs_3_, ...), custom_call_target="tpu_custom_call" | custom-call | flops 4026531840 | bytes 7864320 | tf_op jit(solution)/shard_map/cond/branch_1_fun/project/pallas_call | solution.py:96
  91.1 37.0 %scatter_rows.3 = bf16[4,2,48,1024]{3,2,1,0:T(8,128)(2,1)} custom-call(bf16[8,4,48,1024]{3,2,1,0:T(8,128)(2,1)} %bitcast.60), custom_call_target="tpu_custom_call" | custom-call | tf_op jit(solution)/shard_map/cond/branch_1_fun/scatter_rows/pallas_call | solution.py:351
  128.1 1.9 %copy.51 = bf16[4,48,2,1024]{3,2,1,0:T(2,128)(2,1)S(1)} copy(bf16[4,48,2,1024]{3,1,2,0:T(8,128)(2,1)} %bitcast.66) | data formatting | bytes 1572864 | tf_op jit(solution)/shard_map/cond/branch_1_fun/transpose | solution.py:366
  130.1 0.2 copy.54
  130.3 0.1 pad.6
  130.4 0.2 add_convert_fusion
  130.6 1.4 copy-done.2
  132.0 0.8 fusion.8
  132.8 5.8 %psum.7 = f32[512]{0:T(512)S(1)} all-reduce(f32[512]{0:T(512)S(1)} %get-tuple-element.66), channel_id=1, replica_groups=mesh['dp'=8,'tensor'=4] {'tensor'}, use_global_device_ids=true, to_apply=%region_14.15 | all-reduce | flops 512 | bytes 4096 | tf_op jit(solution)/shard_map/psum | solution.py:433
  138.6 1.9 %fusion.10 = bf16[512,2048]{1,0:T(8,128)(2,1)} fusion(bf16[512,2048]{1,0:T(8,128)(2,1)S(1)} %get-tuple-element.67, f32[2048]{0:T(1024)S(1)} %copy-done.4, f32[512]{0:T(512)S(1)} %add_rsqrt_fusion), kind=kLoop, calls=%fused_computation.26 | loop fusion | flops 4194304 | bytes 4204544 | tf_op jit(solution)/shard_map/convert_element_type | solution.py:435
  (33 shorter events, 0.6 us)
Async XLA Ops:
  11.3 11.2 %copy-start = (bf16[1280,1024]{1,0:T(8,128)(2,1)S(1)}, bf16[1280,1024]{1,0:T(8,128)(2,1)}, u32[]{:S(2)}) copy-start(bf16[1280,1024]{1,0:T(8,128)(2,1)} %param.18) | copy-start | bytes 7864324
  22.6 107.8 %copy-start.3 = (f32[2048]{0:T(1024)S(1)}, f32[2048]{0:T(1024)}, u32[]{:S(2)}) copy-start(f32[2048]{0:T(1024)} %param.19) | copy-start | bytes 24580
  130.4 1.6 %copy-start.2 = (bf16[512,2048]{1,0:T(8,128)(2,1)S(1)}, bf16[512,2048]{1,0:T(8,128)(2,1)}, u32[]{:S(2)}) copy-start(bf16[512,2048]{1,0:T(8,128)(2,1)} %param.20) | copy-start | bytes 6291460
  132.0 6.6 %copy-start.4 = (f32[2048]{0:T(1024)S(1)}, f32[2048]{0:T(1024)}, u32[]{:S(2)}) copy-start(f32[2048]{0:T(1024)} %param.21) | copy-start | bytes 24580
  132.8 7.7 %copy-start.1 = (bf16[512,2048]{1,0:T(8,128)(2,1)}, bf16[512,2048]{1,0:T(8,128)(2,1)S(1)}, u32[]{:S(2)}) copy-start(bf16[512,2048]{1,0:T(8,128)(2,1)S(1)} %get-tuple-element.67) | copy-start | bytes 6291460
where the time goes:
time: 141 us; the launch traced here: 140 us
  Pallas kernels  115 us (82%)
  other arithmetic  9.24 us (7%)
  local copies, waits for them, and re-layouts  8.75 us (6%)
  blocking collectives  5.76 us (4%)
  between operations  2.11 us (1%)
    pallas_call x1, Pallas kernels, gathered_rows(): pl.pallas_call(gather_kernel, in_specs=[pl.BlockSpec(memory_space=pltpu.V...  52.4 us
    pallas_call x1, Pallas kernels, scattered_rows(): pl.pallas_call(scatter_kernel, in_specs=[pl.BlockSpec(memory_space=pltpu....  37 us
    pallas_call x1, Pallas kernels, project(): pl.pallas_call(functools.partial(project_kernel, strides), grid=(shards,)...  13.8 us
    pallas_call x1, Pallas kernels, compact_hidden(): pl.pallas_call(functools.partial(hidden_kernel, per_token), grid=(per_tok...  11.2 us
    psum x1, blocking collectives, per_device(): lax.psum(jnp.sum(embed_values * embed_values, axis=-1), 'tensor')  5.76 us

commit v1 on v0

v1 whole, which is shorter than its diff:
```python
import functools

import jax
import jax.numpy as jnp
from jax import lax
from jax.experimental import pallas as pl
from jax.experimental.pallas import tpu as pltpu
from jax.sharding import PartitionSpec as P

VMEM_LIMIT = 62 * 1024 * 1024
LANES = 128
CHUNK = 256
F32 = jnp.float32
BF16 = jnp.bfloat16


def area_of(grids_ref, s, b):
    return grids_ref[s, b, 0] * grids_ref[s, b, 1]


def segment(grids_ref, routing_ref, s, k):
    count, start = jnp.int32(0), jnp.int32(0)
    for b in range(routing_ref.shape[1]):
        area, offset = area_of(grids_ref, s, b), routing_ref[s, b]
        count = count + jnp.where(offset == k, area, 0)
        start = start + jnp.where(offset < k, area, 0)
    return count, start


def plan_kernel(buckets, grids_ref, routing_ref, which_ref):
    shards, strides = routing_ref.shape

    def widest(e, most):
        sent, filled = jnp.int32(0), jnp.int32(0)
        for k in range(strides):
            sent = sent + area_of(grids_ref, e, k)
            filled = filled + segment(grids_ref, routing_ref, (e + shards - k) % shards, k)[0]
        return jnp.maximum(most, jnp.maximum(sent, filled))

    most = lax.fori_loop(0, shards, widest, jnp.int32(0))
    which = jnp.int32(0)
    for bucket in buckets[:-1]:
        which = which + (most > bucket).astype(jnp.int32)
    which_ref[0] = which


def merge_kernel(
    rows, by_columns,
    grids_ref, routing_ref, patches_ref, gain_ref, bias_ref, first_ref, first_bias_ref, second_ref, second_bias_ref, text_ref,
    out_ref, sums_ref,
    patch_buf, merged, first_buf, second_buf, text_buf, own_pick, acc, gath, proj,
    part, pair_in, cross_out, cross_in, ready_buf, wide, sums_out, sums_in,
    patch_sem, first_sem, second_sem, text_sem,
    line_send, line_recv, pair_send, pair_recv, swap_send, swap_recv, cross_send, cross_recv,
    wide_send, wide_recv, out_send, out_recv, sums_send, sums_recv,
):
    shards, chunks = gath.shape[0], gath.shape[1]
    strides = routing_ref.shape[1]
    groups, piece_rows, piece_cols = part.shape[1:]
    per_group = shards // groups
    length = shards // 2
    per_token, tokens, vit = merged.shape
    cap = tokens // strides
    depth, width = second_buf.shape
    span_width = min(CHUNK, width)
    spans = width // span_width
    ln_rows = LANES
    ln_steps = patch_buf.shape[0] // ln_rows
    ln_tokens = ln_rows // per_token
    seq = text_buf.shape[0]
    feature = text_buf.shape[1]
    top_rows = out_ref.shape[0]

    me = lax.axis_index("dp")
    group = lax.axis_index("tensor")
    place, row = me // 2, me % 2
    other = me + 1 - 2 * row
    core, side = group % 2, group // 2
    mate = 2 * side + 1 - core
    across = group + 2 - 4 * side
    across_mate = mate + 2 - 4 * side
    peers = (mate, across, across_mate)

    barrier = pltpu.get_barrier_semaphore()
    for peer in peers:
        pl.semaphore_signal(barrier, inc=1, device_id={"tensor": peer})

    def greet(i, carry):
        pl.semaphore_signal(barrier, inc=1, device_id={"dp": (me + 1 + i) % shards})
        return carry

    lax.fori_loop(0, shards - 1, greet, 0)

    def patch_copy(i):
        span = pl.ds(pl.multiple_of(i * ln_rows, ln_rows), ln_rows)
        return pltpu.make_async_copy(patches_ref.at[span, :], patch_buf.at[span, :], patch_sem.at[i])

    def first_copy(c):
        span = pl.ds(pl.multiple_of(c * CHUNK, CHUNK), CHUNK)
        return pltpu.make_async_copy(first_ref.at[:, span], first_buf.at[c], first_sem.at[c])

    second_copy = pltpu.make_async_copy(second_ref, second_buf, second_sem)
    text_copy = pltpu.make_async_copy(text_ref, text_buf, text_sem)

    def start_patch(i, carry):
        patch_copy(i).start()
        return carry

    lax.fori_loop(0, ln_steps, start_patch, 0)

    token_row = lax.broadcasted_iota(jnp.int32, (rows, tokens), 0)
    token_gap = lax.broadcasted_iota(jnp.int32, (rows, tokens), 1) - token_row
    picked = jnp.zeros((rows, tokens), jnp.bool_)
    for b in range(strides):
        offset = routing_ref[me, b]
        start = jnp.int32(0)
        for o in range(strides):
            start = start + jnp.where(routing_ref[me, o] < offset, area_of(grids_ref, me, o), 0)
        stop = start + area_of(grids_ref, me, b)
        picked = picked | ((token_row >= start) & (token_row < stop) & (token_gap == b * cap - start))
    own_pick[...] = picked.astype(F32).astype(BF16)

    gain = gain_ref[...][None, :]
    bias = bias_ref[...][None, :]
    line = lax.broadcasted_iota(jnp.int32, (ln_rows, ln_rows), 0)
    wanted = per_token * (line % ln_tokens) + line // ln_tokens
    regroup = (lax.broadcasted_iota(jnp.int32, (ln_rows, ln_rows), 1) == wanted).astype(F32).astype(BF16)

    def norm_rows(i, carry):
        @pl.when(i < chunks)
        def _():
            first_copy(i).start()

        patch_copy(i).wait()
        span = pl.ds(pl.multiple_of(i * ln_rows, ln_rows), ln_rows)
        values = patch_buf[span, :].astype(F32)
        centered = values - jnp.mean(values, axis=-1, keepdims=True)
        variance = jnp.mean(centered * centered, axis=-1, keepdims=True)
        normed = (centered * lax.rsqrt(variance + 1e-06) * gain + bias).astype(BF16)
        sorted_rows = jnp.dot(regroup, normed, preferred_element_type=F32).astype(BF16)
        for j in range(per_token):
            merged[j, pl.ds(pl.multiple_of(i * ln_tokens, ln_tokens), ln_tokens), :] = sorted_rows[j * ln_tokens:(j + 1) * ln_tokens]
        return carry

    lax.fori_loop(0, ln_steps, norm_rows, 0)
    second_copy.start()
    text_copy.start()
    pl.semaphore_wait(barrier, shards - 1 + len(peers))

    def hidden_chunk(c):
        first_copy(c).wait()

        def add(j, carry):
            weight = first_buf[c, pl.ds(pl.multiple_of(j * vit, vit), vit), :]
            term = jnp.dot(merged[j], weight, preferred_element_type=F32)
            acc[...] = jnp.where(j == 0, term, acc[...] + term)
            return carry

        lax.fori_loop(0, per_token, add, 0)
        x = acc[...] + first_bias_ref[pl.ds(pl.multiple_of(c * CHUNK, CHUNK), CHUNK)][None, :]
        hidden = (0.5 * x * (1.0 + lax.erf(x * (0.5 ** 0.5)))).astype(BF16)
        gath[me, c] = jnp.dot(own_pick[...], hidden, preferred_element_type=F32).astype(BF16)

    def line_copy(block, c, way):
        here = gath.at[2 * block + row, c]
        return pltpu.make_async_remote_copy(
            src_ref=here,
            dst_ref=here,
            send_sem=line_send.at[(way + 1) // 2, block, c],
            recv_sem=line_recv.at[block, c],
            device_id={"dp": me + 2 * way},
        )

    def pair_copy(block, c, side_row):
        here = gath.at[2 * block + side_row, c]
        return pltpu.make_async_remote_copy(
            src_ref=here,
            dst_ref=here,
            send_sem=pair_send.at[block, c],
            recv_sem=pair_recv.at[block, c],
            device_id={"dp": other},
        )

    def swap_copy(e, slot):
        return pltpu.make_async_remote_copy(
            src_ref=part.at[e, mate if slot == 0 else across_mate],
            dst_ref=pair_in.at[e, slot],
            send_sem=swap_send.at[slot, e],
            recv_sem=swap_recv.at[slot, e],
            device_id={"tensor": mate},
        )

    def cross_copy(e):
        return pltpu.make_async_remote_copy(
            src_ref=cross_out.at[e],
            dst_ref=cross_in.at[e],
            send_sem=cross_send.at[e],
            recv_sem=cross_recv.at[e],
            device_id={"tensor": across},
        )

    def wide_copy(e, source):
        return pltpu.make_async_remote_copy(
            src_ref=ready_buf.at[e],
            dst_ref=wide.at[source],
            send_sem=wide_send.at[e],
            recv_sem=wide_recv.at[source],
            device_id={"dp": e},
        )

    def place_of(source, sender):
        if by_columns:
            at = ((source % per_group) * groups + sender) * piece_cols
            return pl.ds(0, rows), pl.ds(pl.multiple_of(at, piece_cols), piece_cols)
        return (
            pl.ds(pl.multiple_of(sender * piece_rows, piece_rows), piece_rows),
            pl.ds(pl.multiple_of((source % per_group) * piece_cols, piece_cols), piece_cols),
        )

    def out_copy(source, target, sender):
        return pltpu.make_async_remote_copy(
            src_ref=wide.at[source],
            dst_ref=out_ref.at[place_of(source, sender)],
            send_sem=out_send.at[source],
            recv_sem=out_recv.at[sender, source % per_group],
            device_id={"tensor": target},
        )

    def ready_step(e, at_place, at_row):
        last = jnp.int32(0)
        for k in range(strides):
            source = (e + shards - k) % shards
            away = jnp.abs(source // 2 - at_place) + 1 + jnp.abs(source % 2 - at_row)
            last = jnp.maximum(last, away)
        return last

    def over_shards(body):
        def run(i, carry):
            body((me + 1 + i) % shards)
            return carry

        lax.fori_loop(0, shards, run, 0)

    def project(source, q):
        left = jnp.concatenate([gath[source, c] for c in range(chunks)], axis=1)
        span = pl.ds(pl.multiple_of(q * span_width, span_width), span_width)
        proj[source, :, span] = jnp.dot(left, second_buf[:, span], preferred_element_type=F32).astype(BF16)

    def pick(e):
        at_row = lax.broadcasted_iota(jnp.int32, (rows, rows), 0)
        gap = lax.broadcasted_iota(jnp.int32, (rows, rows), 1) - at_row
        laid = jnp.int32(0)
        total = None
        for k in range(strides):
            source = (e + shards - k) % shards
            count, start = segment(grids_ref, routing_ref, source, k)
            chosen = (at_row >= laid) & (at_row < laid + count) & (gap == start - laid)
            term = jnp.dot(chosen.astype(F32).astype(BF16), proj[source], preferred_element_type=F32)
            total = term if total is None else total + term
            laid = laid + count
        total = total.astype(BF16)
        for g in range(groups):
            if by_columns:
                part[e, g] = total[:, g * piece_cols:(g + 1) * piece_cols]
            else:
                part[e, g] = total[g * piece_rows:(g + 1) * piece_rows]
        for slot in (1, 0):
            swap_copy(e, slot).start()

    def cross(e):
        swap_copy(e, 1).wait_recv()
        cross_out[e] = (part[e, across].astype(F32) + pair_in[e, 1].astype(F32)).astype(BF16)
        cross_copy(e).start()

    def forward(source):
        target = source // per_group

        @pl.when(target == group)
        def _():
            at_rows, at_cols = place_of(source, group)
            out_ref[at_rows, at_cols] = wide[source]

        @pl.when(target != group)
        def _():
            out_copy(source, target, group).start()

    def finish(e):
        swap_copy(e, 0).wait_recv()
        cross_copy(e).wait_recv()
        total = (part[e, group].astype(F32) + pair_in[e, 0].astype(F32) + cross_in[e].astype(F32)).astype(BF16)

        @pl.when(e != me)
        def _():
            ready_buf[e] = total
            wide_copy(e, me).start()

        @pl.when(e == me)
        def _():
            wide[me] = total
            forward(me)

    def row_sums(values):
        squares = values * values
        lanes = squares[:, :LANES]
        for f in range(1, feature // LANES):
            lanes = lanes + squares[:, f * LANES:(f + 1) * LANES]
        return jnp.sum(lanes.T, axis=0, keepdims=True)

    def text_sums():
        text_copy.wait()

        def block(i, carry):
            span = pl.ds(pl.multiple_of(i * LANES, LANES), LANES)
            sums_out[:, span] = row_sums(text_buf[span, :].astype(F32))
            return carry

        lax.fori_loop(0, seq // LANES, block, 0)

    pick_slot = (spans + 1) // 2
    cross_slot = pick_slot + 1

    def slot_step(step, c):
        @pl.when(step == 0)
        def _():
            hidden_chunk(c)

        for way in (1, -1):
            block = place - way * step
            have = (step < length) & (block >= 0) & (block < length)

            @pl.when(have & (step > 0))
            def _(block=block, way=way):
                line_copy(block, c, way).wait_recv()

            @pl.when(have & (place + way >= 0) & (place + way < length))
            def _(block=block, way=way):
                line_copy(block, c, way).start()

            @pl.when(have & ((step > 0) | (way == 1)))
            def _(block=block):
                pair_copy(block, c, row).start()

        @pl.when((step == 1) & (c == 0))
        def _():
            second_copy.wait()

        @pl.when((step == 1) & (c == cross_slot))
        def _():
            text_sums()

        @pl.when((step == length + 1) & (c == 0))
        def _():
            def early(e):
                @pl.when(ready_step(e, place, row) <= length)
                def _():
                    finish(e)

            over_shards(early)

        @pl.when(c < pick_slot)
        def _():
            def unit(i, carry):
                kind, way = i // 2, 1 - 2 * (i % 2)
                away = step - 1 - kind
                block = place - way * away
                fits = (away >= 0) & ((away > 0) | (way == 1)) & (block >= 0) & (block < length)

                @pl.when(fits)
                def _():
                    source = 2 * block + jnp.abs(row - kind)

                    def part_of(h, carry):
                        project(source, 2 * c + h)
                        return carry

                    lax.fori_loop(0, min(2, spans), part_of, 0)

                return carry

            lax.fori_loop(0, 4, unit, 0)

        @pl.when(c == pick_slot)
        def _():
            def now(e):
                @pl.when(ready_step(e, place, row) == step)
                def _():
                    pick(e)

            over_shards(now)

        @pl.when(c == cross_slot)
        def _():
            def now(e):
                @pl.when(ready_step(e, place, row) == step)
                def _():
                    cross(e)

            over_shards(now)

        for way in (1, -1):
            block = place - way * (step - 1)
            have = (step >= 1) & (step <= length) & (block >= 0) & (block < length)

            @pl.when(have & ((step > 1) | (way == 1)))
            def _(block=block):
                pair_copy(block, c, 1 - row).wait_recv()

    def outer(step, carry):
        def inner(c, carry):
            slot_step(step, c)
            return carry

        return lax.fori_loop(0, chunks, inner, carry)

    lax.fori_loop(0, length + 2, outer, 0)

    def receive(source):
        wide_copy(source, source).wait_recv()
        forward(source)

    def settle(i, carry):
        e = (me + 1 + i) % shards

        @pl.when(ready_step(e, place, row) > length)
        def _():
            finish(e)

        source = (me + 2 * shards - 1 - i) % shards

        @pl.when((source != me) & (ready_step(me, source // 2, source % 2) <= length))
        def _():
            receive(source)

        return carry

    lax.fori_loop(0, shards, settle, 0)

    def late(i, carry):
        source = (me + 2 * shards - 1 - i) % shards

        @pl.when((source != me) & (ready_step(me, source // 2, source % 2) > length))
        def _():
            receive(source)

        return carry

    lax.fori_loop(0, shards, late, 0)

    for peer in peers:

        def arrive(c, carry, peer=peer):
            out_copy(group * per_group + c, peer, peer).wait_recv()
            return carry

        lax.fori_loop(0, per_group, arrive, 0)

    filled = jnp.int32(0)
    for k in range(strides):
        filled = filled + segment(grids_ref, routing_ref, (me + shards - k) % shards, k)[0]

    second_bias = second_bias_ref[...][None, :]
    if rows < top_rows:
        out_ref[rows:, :] = text_buf[rows:top_rows, :]

    def splice(i, carry):
        span = pl.ds(pl.multiple_of(i * LANES, LANES), LANES)
        image = (out_ref[span, :].astype(F32) + second_bias).astype(BF16)
        line = lax.broadcasted_iota(jnp.int32, (LANES, feature), 0) + i * LANES
        values = jnp.where(line < filled, image.astype(F32), text_buf[span, :].astype(F32))
        out_ref[span, :] = values.astype(BF16)
        sums_out[:, span] = row_sums(values)
        return carry

    lax.fori_loop(0, top_rows // LANES, splice, 0)

    def sums_copy(peer, sender, i):
        return pltpu.make_async_remote_copy(
            src_ref=sums_out,
            dst_ref=sums_in.at[sender],
            send_sem=sums_send.at[i],
            recv_sem=sums_recv.at[sender],
            device_id={"tensor": peer},
        )

    for i, peer in enumerate(peers):
        sums_copy(peer, group, i).start()

    def drain_line(t, carry):
        block, c = t // chunks, t % chunks
        pair_copy(block, c, row).wait_send()

        @pl.when((block <= place) & (place < length - 1))
        def _():
            line_copy(block, c, 1).wait_send()

        @pl.when((block >= place) & (place > 0))
        def _():
            line_copy(block, c, -1).wait_send()

        return carry

    lax.fori_loop(0, length * chunks, drain_line, 0)

    def drain(e):
        for slot in (1, 0):
            swap_copy(e, slot).wait_send()
        cross_copy(e).wait_send()

        @pl.when(e != me)
        def _():
            wide_copy(e, me).wait_send()

        @pl.when(e // per_group != group)
        def _():
            out_copy(e, e // per_group, group).wait_send()

    over_shards(drain)
    total = sums_out[...]
    for i, peer in enumerate(peers):
        copy = sums_copy(peer, peer, i)
        copy.wait_recv()
        copy.wait_send()
        total = total + sums_in[peer]
    sums_ref[...] = total


def merge(rows, call_id, shards, groups, grids, routing, patches, norm_gain, norm_bias, first_weight, first_bias, second_weight, second_bias, text_embeds):
    patch_rows, vit = patches.shape
    per_token = first_weight.shape[0] // vit
    tokens = patch_rows // per_token
    hidden_width = first_weight.shape[1]
    chunks = hidden_width // CHUNK
    depth, width = second_weight.shape
    seq, feature = text_embeds.shape
    length = shards // 2
    by_columns = width % (groups * LANES) == 0
    piece = (rows, width // groups) if by_columns else (rows // groups, width)
    per_group = shards // groups
    dma = pltpu.SemaphoreType.DMA
    smem = pl.BlockSpec(memory_space=pltpu.SMEM)
    vmem = pl.BlockSpec(memory_space=pltpu.VMEM)
    anywhere = pl.BlockSpec(memory_space=pl.ANY)
    block = pltpu.VMEM((shards,) + piece, BF16)
    return pl.pallas_call(
        functools.partial(merge_kernel, rows, by_columns),
        in_specs=[smem, smem, anywhere, vmem, vmem, anywhere, vmem, anywhere, vmem, anywhere],
        out_specs=[vmem, vmem],
        out_shape=[
            jax.ShapeDtypeStruct((tokens, feature), BF16),
            jax.ShapeDtypeStruct((1, seq), F32),
        ],
        scratch_shapes=[
            pltpu.VMEM((patch_rows, vit), BF16),
            pltpu.VMEM((per_token, tokens, vit), BF16),
            pltpu.VMEM((chunks, first_weight.shape[0], CHUNK), BF16),
            pltpu.VMEM((depth, width), BF16),
            pltpu.VMEM((seq, feature), BF16),
            pltpu.VMEM((rows, tokens), BF16),
            pltpu.VMEM((tokens, CHUNK), F32),
            pltpu.VMEM((shards, chunks, rows, CHUNK), BF16),
            pltpu.VMEM((shards, rows, width), BF16),
            pltpu.VMEM((shards, groups) + piece, BF16),
            pltpu.VMEM((shards, 2) + piece, BF16),
            block, block, block, block,
            pltpu.VMEM((1, seq), F32),
            pltpu.VMEM((groups, 1, seq), F32),
            dma((patch_rows // LANES,)), dma((chunks,)), dma, dma,
            dma((2, length, chunks)), dma((length, chunks)), dma((length, chunks)), dma((length, chunks)),
            dma((2, shards)), dma((2, shards)), dma((shards,)), dma((shards,)),
            dma((shards,)), dma((shards,)), dma((shards,)), dma((groups, per_group)),
            dma((groups - 1,)), dma((groups,)),
        ],
        compiler_params=pltpu.CompilerParams(
            collective_id=call_id, has_side_effects=True, vmem_limit_bytes=VMEM_LIMIT
        ),
        name="merge_%d" % rows,
    )(grids, routing, patches, norm_gain, norm_bias, first_weight, first_bias, second_weight, second_bias, text_embeds)


def scale_kernel(total_width, top_blocks, top_ref, text_ref, sums_ref, gain_ref, out_ref, normed_ref):
    rows = out_ref.shape[0]
    scale = lax.rsqrt(sums_ref[...] / total_width + 1e-06)
    scale = jnp.broadcast_to(scale, (LANES, rows)).T
    upper = pl.program_id(0) < top_blocks
    gain = gain_ref[...][None, :]
    for f in range(out_ref.shape[1] // LANES):
        span = slice(f * LANES, (f + 1) * LANES)
        values = jnp.where(upper, top_ref[:, span].astype(F32), text_ref[:, span].astype(F32))
        out_ref[:, span] = values.astype(BF16)
        normed_ref[:, span] = (values * scale * gain[:, span]).astype(BF16)


def scale_rows(top, text_embeds, sums, final_gain, groups):
    seq, feature = text_embeds.shape
    top_blocks = top.shape[0] // LANES
    block = pl.BlockSpec((LANES, feature), lambda i: (i, 0))
    return pl.pallas_call(
        functools.partial(scale_kernel, feature * groups, top_blocks),
        grid=(seq // LANES,),
        in_specs=[
            pl.BlockSpec((LANES, feature), lambda i: (jnp.minimum(i, top_blocks - 1), 0)),
            block,
            pl.BlockSpec((1, LANES), lambda i: (0, i)),
            pl.BlockSpec((feature,), lambda i: (0,)),
        ],
        out_specs=[block, block],
        out_shape=[jax.ShapeDtypeStruct((seq, feature), BF16)] * 2,
        compiler_params=pltpu.CompilerParams(vmem_limit_bytes=VMEM_LIMIT),
        name="scale_rows",
    )(top, text_embeds, sums, final_gain)


def bucket_sizes(slots, width, groups):
    step = slots // 16 if width % (groups * LANES) == 0 else slots // 4
    return tuple(b for b in range(slots // 2 + step, slots + 1, step) if b <= slots * 13 // 16 or b == slots)


def per_device(
    patches,
    norm_gain,
    norm_bias,
    first_weight,
    first_bias,
    second_weight,
    second_bias,
    text_embeds,
    final_gain,
    image_grids,
    routing,
):
    shards = lax.axis_size("dp")
    groups = lax.axis_size("tensor")
    slots = patches.shape[0] * patches.shape[1] // first_weight.shape[0]
    buckets = BUCKETS(slots, second_weight.shape[1], groups)
    smem = pl.BlockSpec(memory_space=pltpu.SMEM)
    which = pl.pallas_call(
        functools.partial(plan_kernel, buckets),
        in_specs=[smem, smem],
        out_specs=smem,
        out_shape=jax.ShapeDtypeStruct((1,), jnp.int32),
        name="plan",
    )(image_grids, routing)

    def branch(rows, call_id):
        return lambda: merge(
            rows, call_id, shards, groups, image_grids, routing, patches, norm_gain, norm_bias,
            first_weight, first_bias, second_weight, second_bias, text_embeds,
        )

    top, sums = lax.switch(which[0], [branch(rows, i) for i, rows in enumerate(buckets)])
    return tuple(scale_rows(top, text_embeds, sums, final_gain, groups))


BUCKETS = bucket_sizes


def solution(mesh):
    placed = (
        P("dp", None),
        P(),
        P(),
        P(None, "tensor"),
        P("tensor"),
        P("tensor", "dp"),
        P("tensor"),
        P("dp", "tensor"),
        P("tensor"),
        P(),
        P(),
    )
    return jax.shard_map(
        per_device,
        mesh=mesh,
        in_specs=placed,
        out_specs=(P("dp", "tensor"), P("dp", "tensor")),
        check_vma=False,
    )
```

time: 141 us -> 102 us (0.72)
  Pallas kernels: 115 us -> 93.6 us
  other arithmetic: 9.24 us -> 0 us
  blocking collectives: 5.76 us -> 0 us
  local copies, waits for them, and re-layouts: 8.75 us -> 5.46 us
    pallas_call x4 -> x3, Pallas kernels: 115 us -> 93.6 us  [the longest x1 86.8 us: merge(): pl.pallas_call(functools.partial(merge_kernel, rows, by_columns), in_spec...]
    psum x1 -> x0, blocking collectives: 5.76 us -> none  [per_device(): lax.psum(jnp.sum(embed_values * embed_values, axis=-1), 'tensor')]
    another operation x1 -> x2, local copies, waits for them, and re-layouts: 0.19 us -> 2.73 us
    slice x15 -> x0, local copies, waits for them, and re-layouts: 2.29 us -> none  [the longest x1 0.81 us: image_part(): gathered = gathered_rows(hidden[:rows], 2 * call_id)]
    convert_element_type x3 -> x0, other arithmetic: 2.09 us -> none  [the longest x1 1.87 us: per_device(): (embed_values * scale_rows[:, None] * final_gain).astype(jnp.bfloat16)]
    reduce_max x2 -> x0, other arithmetic: 2.06 us -> none  [per_device(): most = jnp.maximum(jnp.max(jnp.sum(counts, axis=1)), jnp.max(filled))]
    sub x2 -> x0, local copies, waits for them, and re-layouts: 2 us -> none  [the longest x1 1.19 us: image_part(): jnp.sum(jnp.where(live, slot_ids * rows + source_starts[:, None, :] + ins...]
    transpose x1 -> x0, local copies, waits for them, and re-layouts: 1.94 us -> none  [scattered_rows(): return out.transpose(0, 2, 1, 3).reshape(groups * rows, -1)]
where the time goes in v1:
time: 102 us; the launch traced here: 101 us
  Pallas kernels  93.6 us (92%)
  local copies, waits for them, and re-layouts  5.46 us (5%)
  between operations  1.28 us (1%)
    pallas_call x1, Pallas kernels, merge(): pl.pallas_call(functools.partial(merge_kernel, rows, by_columns), in_spec...  86.8 us
    pallas_call x1, Pallas kernels, scale_rows(): pl.pallas_call(functools.partial(scale_kernel, feature * groups, top_bloc...  4.76 us
    another operation x2, local copies, waits for them, and re-layouts  2.73 us
    unnamed x2, local copies, waits for them, and re-layouts  2.73 us
    pallas_call x1, Pallas kernels, per_device(): pl.pallas_call(functools.partial(plan_kernel, buckets), in_specs=[smem, s...  2.08 us

profile of v1, /device:TPU:0, one launch (start us, length us, event | category | flops | bytes accessed | tf_op | source)
XLA Modules:
  0.0 100.6 jit_solution(15937829052290612333)
XLA Ops:
  0.6 1.3 %copy.14.routing_ref = s32[8,4]{1,0:T(8,128)} copy(s32[8,4]{0,1:T(4,128)} %param.27) | data formatting | bytes 256 | tf_op args[10]
  2.0 1.4 %copy.13.grids_ref = s32[8,4,2]{2,1,0:T(4,128)} copy(s32[8,4,2]{0,2,1:T(2,128)} %param.26) | data formatting | bytes 512 | tf_op args[9]
  3.4 2.1 %plan.1 = s32[1]{0:T(128)} custom-call(s32[8,4,2]{2,1,0:T(4,128)} %copy.13.grids_ref, s32[8,4]{1,0:T(8,128)} %copy.14.routing_ref), custom_call_target="tpu_custom_call" | custom-call | tf_op jit(solution)/shard_map/plan/pallas_call | solution.py:636
  6.1 89.8 %conditional.1 = ((bf16[256,2048]{1,0:T(8,128)(2,1)S(1)}, f32[1,512]{1,0:T(1,128)S(1)})) conditional(s32[]{:T(128)} %bitcast, (s32[8,4,2]{0,2,1:T(2,128)}, s32[8,4]{0,1:T(4,128)}, bf16[1024,1280]{1,0:T(8,128)(2,1)}, f32[1280]{0:T(1024)}, f32[1280]{0:T(1024)}, /*index=5*/bf16[5120,1280]{1,0:T(8,128)(2,1)}, ...), branch_computations={%region_0.0_spmd, %region_1.0_spmd, %region_2.0_spmd, %region_3.0_... | conditional | bytes 776 | solution.py:650
  6.1 1.4 %copy.20.routing_ref = s32[8,4]{1,0:T(8,128)} copy(s32[8,4]{0,1:T(4,128)} %get-tuple-element.207) | data formatting | bytes 256 | tf_op jit(solution)/shard_map
  7.5 1.4 %copy.19.grids_ref = s32[8,4,2]{2,1,0:T(4,128)} copy(s32[8,4,2]{0,2,1:T(2,128)} %get-tuple-element.206) | data formatting | bytes 512 | tf_op jit(solution)/shard_map
  8.9 86.8 %merge_176.1 = (bf16[256,2048]{1,0:T(8,128)(2,1)S(1)}, f32[1,512]{1,0:T(1,128)S(1)}) custom-call(s32[8,4,2]{2,1,0:T(4,128)} %copy.19.grids_ref, s32[8,4]{1,0:T(8,128)} %copy.20.routing_ref, bf16[1024,1280]{1,0:T(8,128)(2,1)} %get-tuple-element.142.patches_ref, f32[1280]{0:T(1024)} %get-tuple-element.143.gain_ref, f32[1280]{0:T(1024)} %get-tuple-element.144.bias_ref, ...), custom_call_target="tpu_custom_call" | custom-call | tf_op jit(solution)/shard_map/cond/branch_2_fun/merge_176/pallas_call | solution.py:544
  95.9 4.8 %scale_rows.1 = (bf16[512,2048]{1,0:T(8,128)(2,1)}, bf16[512,2048]{1,0:T(8,128)(2,1)}) custom-call(bf16[256,2048]{1,0:T(8,128)(2,1)S(1)} %get-tuple-element.184.top_ref, bf16[512,2048]{1,0:T(8,128)(2,1)} %text_ref.1, f32[1,512]{1,0:T(1,128)S(1)} %get-tuple-element.185.sums_ref, f32[2048]{0:T(1024)} %gain_ref.1), custom_call_target="tpu_custom_call" | custom-call | tf_op jit(solution)/shard_map/scale_rows/pallas_call | solution.py:597
